TPU v7x, 32 devices: a whole 2x2x4 slice. The times are simulated.
32 devices in a mesh: blk: 8 (over z, x), tgt: 4 (over y, core).
Axes of the slice: x: 2, y: 2, z: 4, core: 2. Of those that a mesh axis runs over, the one named last changes fastest.
Arguments:
- sources: float32 [8192, 128], P('blk'), may hold values from -0.5 to 0.5, as said below
- targets: float32 [8192, 128], P(('blk', 'tgt')), may hold values from -0.5 to 0.5, as said below
- duals_init: float32 [8192], P(('blk', 'tgt')), may hold values from -1.5 to 1.5
Outputs:
- source_duals: float32 [8192], P('blk')
- target_duals: float32 [8192], P(('blk', 'tgt'))
Inputs may be any that keep to these rules, and one draw needn't show every extreme that they name: `sources`: coordinates of the source points. `targets`: coordinates of the target points.
All inputs are finite; a program needn't handle non-finite values.
Results may differ from a plain program's by a relative error of at most 0.0001.
Values sent between devices are 32-bit elements; how exact they have to be, the bound alone decides.
A program may use at most 64 MiB of HBM per device.

v0:
```python
import jax
import jax.numpy as jnp
from jax import lax
from jax.sharding import PartitionSpec as P

ITERS = 2
EPS = 0.05


def cost_of(left, left_norm, right, right_norm):
    cross = jnp.dot(
        left, right.T, preferred_element_type=jnp.float32, precision=lax.Precision.HIGHEST
    )
    return left_norm[:, None] + right_norm[None, :] - 2.0 * cross


def body(sources, targets, duals_init):
    src_norm = jnp.sum(sources * sources, axis=1)
    rows_here = sources.shape[0]
    cols_here = targets.shape[0]
    total_dst = cols_here * lax.axis_size("blk") * lax.axis_size("tgt")
    total_src = rows_here * lax.axis_size("blk")
    target_pots = duals_init
    source_pots = jnp.zeros_like(src_norm)
    group_rows = lax.all_gather(targets, "blk", axis=0, tiled=True)
    group_norm = jnp.sum(group_rows * group_rows, axis=1)
    cost_tile = cost_of(sources, src_norm, group_rows, group_norm)
    for repeat in range(ITERS):
        group_pots = lax.all_gather(target_pots, "blk", axis=0, tiled=True)
        scores = (group_pots[None, :] - cost_tile) / EPS
        maxima = jnp.max(scores, axis=1)
        totals = jnp.sum(jnp.exp(scores - maxima[:, None]), axis=1)
        highest = lax.pmax(maxima, "tgt")
        totals = lax.psum(totals * jnp.exp(maxima - highest), "tgt")
        maxima = highest
        source_pots = EPS * -jnp.log(jnp.float32(total_dst)) - EPS * (maxima + jnp.log(totals))
        col_scores = (source_pots[:, None] - cost_tile) / EPS
        col_high = lax.pmax(jnp.max(col_scores, axis=0), "blk")
        col_part = jnp.sum(jnp.exp(col_scores - col_high[None, :]), axis=0)
        col_total = lax.psum_scatter(col_part, "blk", scatter_dimension=0, tiled=True)
        own_high = lax.dynamic_slice_in_dim(
            col_high, lax.axis_index("blk") * cols_here, cols_here, 0
        )
        target_pots = EPS * -jnp.log(jnp.float32(total_src)) - EPS * (own_high + jnp.log(col_total))
    return (source_pots, target_pots)


def solution(mesh):
    return jax.shard_map(
        body,
        mesh=mesh,
        in_specs=(P("blk", None), P(("blk", "tgt"), None), P(("blk", "tgt"))),
        out_specs=(P("blk"), P(("blk", "tgt"))),
        check_vma=False,
    )
```

profile of v0, /device:TPU:0, one launch (start us, length us, event | category | flops | bytes accessed | tf_op | source)
XLA Modules:
  0.0 220.8 jit_solution(6186228106651673261)
XLA Ops:
  7.2 0.0 all-gather.4.cloned.1.call-start
  7.2 0.7 all-gather.4.cloned.1.call-update
  7.9 1.2 dynamic-slice
  9.8 22.5 %all-gather = f32[8,1,256]{2,1,0:T(1,128)S(1)} all-gather(f32[1,1,256]{2,1,0:T(1,128)} %bitcast.12), channel_id=1, replica_groups=mesh['blk'=8,'tgt'=4] {'blk'}, dimensions={0}, use_global_device_ids=true | all-gather | bytes 9216 | tf_op jit(solution)/shard_map/all_gather | solution.py:29
  32.3 1.2 multiply_reduce_fusion.1
  33.6 19.5 %all-gather.4.cloned.1.call-done = f32[2048,128]{1,0:T(8,128)} async-done(((f32[256,128]{1,0:T(8,128)}), f32[2048,128]{1,0:T(8,128)}) %all-gather.4.cloned.1.call-update) | async-done | bytes 1048592 | tf_op jit(solution)/shard_map/all_gather | solution.py:25
  53.1 1.6 multiply_reduce_fusion
  54.7 11.5 %fusion = (f32[1024]{0:T(1024)S(1)}, f32[1024,2048]{1,0:T(8,128)}) fusion(f32[2048]{0:T(1024)S(1)} %bitcast.9, f32[1024,128]{1,0:T(8,128)} %param.3, f32[2048,128]{1,0:T(8,128)} %all-gather.4.cloned.1.call-done, f32[2048]{0:T(1024)S(1)} %multiply_reduce_fusion, f32[1024]{0:T(1024)S(1)} %multiply_reduce_fusion.1), kind=kOutput, calls=%fused_computation.9 | convolution fusion | flops 3233807360 | bytes 9986048 | tf_op jit(solution)/shard_map/dot_general | solution.py:11
  66.2 5.6 %pmax.28 = f32[1024]{0:T(1024)S(1)} all-reduce(f32[1024]{0:T(1024)S(1)} %get-tuple-element.2), channel_id=1, replica_groups=mesh['blk'=8,'tgt'=4] {'tgt'}, use_global_device_ids=true, to_apply=%region_3.0 | all-reduce | flops 1024 | bytes 8192 | tf_op jit(solution)/shard_map/pmax | solution.py:33
  71.8 4.5 %exponential_reduce_fusion.3 = f32[1024]{0:T(1024)S(1)} fusion(f32[1024,2048]{1,0:T(8,128)} %get-tuple-element.3, f32[1024]{0:T(1024)S(1)} %get-tuple-element.2, f32[2048]{0:T(1024)S(1)} %bitcast.10), kind=kLoop, calls=%fused_computation.6 | loop fusion | flops 8387584 | bytes 8404992 | tf_op jit(solution)/shard_map/reduce_sum | solution.py:32
  76.4 6.6 %psum.14 = f32[1024]{0:T(1024)S(1)} all-reduce(f32[1024]{0:T(1024)S(1)} %exponential_multiply_fusion.1), channel_id=1, replica_groups=mesh['blk'=8,'tgt'=4] {'tgt'}, use_global_device_ids=true, to_apply=%region_5.0 | all-reduce | flops 1024 | bytes 8192 | tf_op jit(solution)/shard_map/psum | solution.py:34
  83.0 4.3 %fusion.1 = f32[2048]{0:T(1024)S(1)} fusion(f32[1024,2048]{1,0:T(8,128)} %get-tuple-element.3, f32[1024]{0:T(1024)S(1)} %multiply_subtract_fusion.2), kind=kLoop, calls=%fused_computation.10 | loop fusion | flops 6289408 | bytes 8400896 | tf_op jit(solution)/shard_map/reduce_max | solution.py:38
  87.3 19.4 %pmax.29 = f32[2048]{0:T(1024)S(1)} all-reduce(f32[2048]{0:T(1024)S(1)} %fusion.1), channel_id=1, replica_groups=mesh['blk'=8,'tgt'=4] {'blk'}, use_global_device_ids=true, to_apply=%region_7.0 | all-reduce | flops 2048 | bytes 16384 | tf_op jit(solution)/shard_map/pmax | solution.py:38
  106.7 4.5 %exponential_reduce_fusion.2 = f32[2048]{0:T(1024)S(1)} fusion(f32[1024,2048]{1,0:T(8,128)} %get-tuple-element.3, f32[2048]{0:T(1024)S(1)} %pmax.29, f32[1024]{0:T(1024)S(1)} %multiply_subtract_fusion.2), kind=kLoop, calls=%fused_computation.4 | loop fusion | flops 8386560 | bytes 8409088 | tf_op jit(solution)/shard_map/reduce_sum | solution.py:39
  111.2 17.4 %all-reduce = f32[2048]{0:T(1024)S(1)} all-reduce(f32[2048]{0:T(1024)S(1)} %exponential_reduce_fusion.2), channel_id=2, replica_groups=mesh['blk'=8,'tgt'=4] {'blk'}, use_global_device_ids=true, to_apply=%region_9.0.clone | all-reduce | flops 2048 | bytes 16384
  128.6 0.1 fusion.9
  128.7 18.2 %all-gather.1 = f32[8,1,256]{2,1,0:T(1,128)S(1)} all-gather(f32[1,1,256]{2,1,0:T(1,128)S(1)} %bitcast.11), channel_id=1, replica_groups=mesh['blk'=8,'tgt'=4] {'blk'}, dimensions={0}, use_global_device_ids=true | all-gather | bytes 9216 | tf_op jit(solution)/shard_map/all_gather | solution.py:29
  147.0 4.3 %fusion.2 = f32[1024]{0:T(1024)S(1)} fusion(f32[1024,2048]{1,0:T(8,128)} %get-tuple-element.3, f32[2048]{0:T(1024)S(1)} %bitcast.7), kind=kLoop, calls=%fused_computation.11 | loop fusion | flops 6290432 | bytes 8400896 | tf_op jit(solution)/shard_map/reduce_max | solution.py:31
  151.3 4.5 %exponential_reduce_fusion.1 = f32[1024]{0:T(1024)S(1)} fusion(f32[1024,2048]{1,0:T(8,128)} %get-tuple-element.3, f32[1024]{0:T(1024)S(1)} %fusion.2, f32[2048]{0:T(1024)S(1)} %bitcast.8), kind=kLoop, calls=%fused_computation.2 | loop fusion | flops 8387584 | bytes 8404992 | tf_op jit(solution)/shard_map/reduce_sum | solution.py:32
  155.8 5.7 %pmax.30 = f32[1024]{0:T(1024)S(1)} all-reduce(f32[1024]{0:T(1024)S(1)} %fusion.2), channel_id=1, replica_groups=mesh['blk'=8,'tgt'=4] {'tgt'}, use_global_device_ids=true, to_apply=%region_11.0 | all-reduce | flops 1024 | bytes 8192 | tf_op jit(solution)/shard_map/pmax | solution.py:33
  161.5 6.3 %psum.15 = f32[1024]{0:T(1024)S(1)} all-reduce(f32[1024]{0:T(1024)S(1)} %exponential_multiply_fusion), channel_id=1, replica_groups=mesh['blk'=8,'tgt'=4] {'tgt'}, use_global_device_ids=true, to_apply=%region_13.0 | all-reduce | flops 1024 | bytes 8192 | tf_op jit(solution)/shard_map/psum | solution.py:34
  167.7 0.0 copy-start
  167.7 4.3 %fusion.3 = f32[2048]{0:T(1024)S(1)} fusion(f32[1024,2048]{1,0:T(8,128)} %get-tuple-element.3, f32[1024]{0:T(1024)S(1)} %multiply_subtract_fusion.1), kind=kLoop, calls=%fused_computation.12 | loop fusion | flops 6289408 | bytes 8400896 | tf_op jit(solution)/shard_map/reduce_max | solution.py:38
  172.0 17.4 %pmax.31 = f32[2048]{0:T(1024)S(1)} all-reduce(f32[2048]{0:T(1024)S(1)} %fusion.3), channel_id=1, replica_groups=mesh['blk'=8,'tgt'=4] {'blk'}, use_global_device_ids=true, to_apply=%region_15.0 | all-reduce | flops 2048 | bytes 16384 | tf_op jit(solution)/shard_map/pmax | solution.py:38
  189.4 4.5 %exponential_reduce_fusion = f32[2048]{0:T(1024)S(1)} fusion(f32[1024,2048]{1,0:T(8,128)} %get-tuple-element.3, f32[2048]{0:T(1024)S(1)} %pmax.31, f32[1024]{0:T(1024)S(1)} %multiply_subtract_fusion.1), kind=kLoop, calls=%fused_computation | loop fusion | flops 8386560 | bytes 8409088 | tf_op jit(solution)/shard_map/reduce_sum | solution.py:39
  193.9 0.0 copy-done
  193.9 19.4 %all-reduce.1 = f32[2048]{0:T(1024)S(1)} all-reduce(f32[2048]{0:T(1024)S(1)} %exponential_reduce_fusion), channel_id=3, replica_groups=mesh['blk'=8,'tgt'=4] {'blk'}, use_global_device_ids=true, to_apply=%region_17.0.clone | all-reduce | flops 2048 | bytes 16384
  213.3 0.7 fusion.6
  (4 shorter events, 0.0 us)
Async XLA Ops:
  7.2 46.0 %all-gather.4.cloned.1.call-start = ((), (), s32[]{:S(2)}) async-start(), calls=%async_computation | async-start | bytes 1179648 | tf_op jit(solution)/shard_map/all_gather | solution.py:25
  167.7 26.2 %copy-start = (f32[1024]{0:T(1024)}, f32[1024]{0:T(1024)S(1)}, u32[]{:S(2)}) copy-start(f32[1024]{0:T(1024)S(1)} %multiply_subtract_fusion.1) | copy-start | bytes 12292
Sparse Core Ops, SparseCore 0:
  10.1 42.9 all-gather.3
where the time goes:
time: 221 us
  blocking collectives  139 us (63%)
  other arithmetic  34.5 us (16%)
  waiting for transfers between devices  20.2 us (9%)
  between operations  14.8 us (7%)
  matrix products  11.5 us (5%)
    all_gather x2, blocking collectives, body(): group_pots = lax.all_gather(target_pots, 'blk', axis=0, tiled=True)  40.8 us
    unnamed x2, blocking collectives  36.8 us
    pmax x2, blocking collectives, body(): col_high = lax.pmax(jnp.max(col_scores, axis=0), 'blk')  36.8 us
    all_gather x1, waiting for transfers between devices, body(): group_rows = lax.all_gather(targets, 'blk', axis=0, tiled=True)  19.5 us
    psum x2, blocking collectives, body(): totals = lax.psum(totals * jnp.exp(maxima - highest), 'tgt')  12.9 us
    dot_general x1, matrix products, cost_of(): jnp.dot(left, right.T, preferred_element_type=jnp.float32, precision=lax....  11.5 us
    pmax x2, blocking collectives, body(): highest = lax.pmax(maxima, 'tgt')  11.3 us
    reduce_sum x2, other arithmetic, body(): totals = jnp.sum(jnp.exp(scores - maxima[:, None]), axis=1)  9.01 us
  transfers between devices with their start and end apart: 1, of which 1 were waited for; matrix products, arithmetic and copies ran while one was open for 1% of the time, Pallas kernels for 0%

commit v1 on v0

--- a/solution.py
+++ b/solution.py
@@ -26,7 +26,14 @@
     group_norm = jnp.sum(group_rows * group_rows, axis=1)
     cost_tile = cost_of(sources, src_norm, group_rows, group_norm)
     for repeat in range(ITERS):
-        group_pots = lax.all_gather(target_pots, "blk", axis=0, tiled=True)
+        size = lax.axis_size("blk")
+        route = [(i, (i + 1) % size) for i in range(size)]
+        parts = [target_pots]
+        for far in range(1, size):
+            parts = [lax.ppermute(parts[0], "blk", route), *parts]
+        whole = jnp.concatenate(parts, axis=0)
+        shift = (lax.axis_index("blk") + 1) * parts[-1].shape[0]
+        group_pots = jnp.roll(whole, shift, axis=0)
         scores = (group_pots[None, :] - cost_tile) / EPS
         maxima = jnp.max(scores, axis=1)
         totals = jnp.sum(jnp.exp(scores - maxima[:, None]), axis=1)

time: 221 us -> 248 us (1.12)
  waiting for transfers between devices: 20.2 us -> 83.1 us
  blocking collectives: 139 us -> 97.8 us
  starting transfers between devices: 0.04 us -> 3.86 us
    ppermute x0 -> x14, waiting for transfers between devices: none -> 82.4 us  [body(): parts = [lax.ppermute(parts[0], 'blk', route), *parts]]
    all_gather x2 -> x0, blocking collectives: 40.8 us -> none  [body(): group_pots = lax.all_gather(target_pots, 'blk', axis=0, tiled=True)]
    all_gather x1, waiting for transfers between devices: 19.5 us -> 0.01 us  [body(): group_rows = lax.all_gather(targets, 'blk', axis=0, tiled=True)]
    ppermute x0 -> x14, starting transfers between devices: none -> 3.82 us  [body(): parts = [lax.ppermute(parts[0], 'blk', route), *parts]]
  transfers between devices with their start and end apart: 1 -> 15, of which waited for: 1 -> 14; matrix products, arithmetic and copies ran while one was open for 1% -> 1% of each run, Pallas kernels for 0% -> 0%
where the time goes in v1:
time: 248 us
  blocking collectives  97.8 us (39%)
  waiting for transfers between devices  83.1 us (34%)
  other arithmetic  34.7 us (14%)
  between operations  14.9 us (6%)
  matrix products  11.5 us (5%)
  starting transfers between devices  3.86 us (2%)
    ppermute x14, waiting for transfers between devices, body(): parts = [lax.ppermute(parts[0], 'blk', route), *parts]  82.4 us
    unnamed x2, blocking collectives  38 us
    pmax x2, blocking collectives, body(): col_high = lax.pmax(jnp.max(col_scores, axis=0), 'blk')  35.5 us
    psum x2, blocking collectives, body(): totals = lax.psum(totals * jnp.exp(maxima - highest), 'tgt')  13 us
    dot_general x1, matrix products, cost_of(): jnp.dot(left, right.T, preferred_element_type=jnp.float32, precision=lax....  11.5 us
    pmax x2, blocking collectives, body(): highest = lax.pmax(maxima, 'tgt')  11.3 us
    reduce_sum x2, other arithmetic, body(): totals = jnp.sum(jnp.exp(scores - maxima[:, None]), axis=1)  9.01 us
    reduce_sum x2, other arithmetic, body(): col_part = jnp.sum(jnp.exp(col_scores - col_high[None, :]), axis=0)  9.01 us
  transfers between devices with their start and end apart: 15, of which 14 were waited for; matrix products, arithmetic and copies ran while one was open for 1% of the time, Pallas kernels for 0%

profile of v1, /device:TPU:0, one launch (start us, length us, event | category | flops | bytes accessed | tf_op | source)
XLA Modules:
  0.0 247.8 jit_solution(13663073381564210351)
XLA Ops:
  7.2 0.0 all-gather.2.cloned.1.call-start
  7.2 0.7 all-gather.2.cloned.1.call-update
  7.9 3.0 %collective-permute-start = (f32[256]{0:T(256)}, f32[256]{0:T(256)S(1)}, u32[]{:S(2)}, u32[]{:S(2)}) collective-permute-start(f32[256]{0:T(256)} %param.7), channel_id=1, source_target_pairs={{0,4},{4,8},{8,12},{12,16},{16,20},{20,24},{24,28},{28,0},{1,5},{5... | collective-permute-start | bytes 3080 | tf_op jit(solution)/shard_map/ppermute | solution.py:33
  10.9 4.8 %collective-permute-done = f32[256]{0:T(256)S(1)} collective-permute-done((f32[256]{0:T(256)}, f32[256]{0:T(256)S(1)}, u32[]{:S(2)}, u32[]{:S(2)}) %collective-permute-start) | collective-permute-done | bytes 1056 | tf_op jit(solution)/shard_map/ppermute | solution.py:33
  15.7 0.0 collective-permute-start.1
  15.7 6.3 %collective-permute-done.1 = f32[256]{0:T(256)S(1)} collective-permute-done((f32[256]{0:T(256)S(1)}, f32[256]{0:T(256)S(1)}, u32[]{:S(2)}, u32[]{:S(2)}) %collective-permute-start.1) | collective-permute-done | bytes 1056 | tf_op jit(solution)/shard_map/ppermute | solution.py:33
  22.0 0.0 collective-permute-start.2
  22.0 6.3 %collective-permute-done.2 = f32[256]{0:T(256)S(1)} collective-permute-done((f32[256]{0:T(256)S(1)}, f32[256]{0:T(256)S(1)}, u32[]{:S(2)}, u32[]{:S(2)}) %collective-permute-start.2) | collective-permute-done | bytes 1056 | tf_op jit(solution)/shard_map/ppermute | solution.py:33
  28.3 0.0 collective-permute-start.3
  28.3 6.3 %collective-permute-done.3 = f32[256]{0:T(256)S(1)} collective-permute-done((f32[256]{0:T(256)S(1)}, f32[256]{0:T(256)S(1)}, u32[]{:S(2)}, u32[]{:S(2)}) %collective-permute-start.3) | collective-permute-done | bytes 1056 | tf_op jit(solution)/shard_map/ppermute | solution.py:33
  34.5 1.2 multiply_reduce_fusion.1
  35.8 5.0 %collective-permute-done.4 = f32[256]{0:T(256)S(1)} collective-permute-done((f32[256]{0:T(256)S(1)}, f32[256]{0:T(256)S(1)}, u32[]{:S(2)}, u32[]{:S(2)}) %collective-permute-start.4) | collective-permute-done | bytes 1056 | tf_op jit(solution)/shard_map/ppermute | solution.py:33
  40.8 6.3 %collective-permute-done.5 = f32[256]{0:T(256)S(1)} collective-permute-done((f32[256]{0:T(256)S(1)}, f32[256]{0:T(256)S(1)}, u32[]{:S(2)}, u32[]{:S(2)}) %collective-permute-start.5) | collective-permute-done | bytes 1056 | tf_op jit(solution)/shard_map/ppermute | solution.py:33
  47.1 0.0 collective-permute-start.6
  47.1 1.2 dynamic-slice
  49.0 4.4 %collective-permute-done.6 = f32[256]{0:T(256)S(1)} collective-permute-done((f32[256]{0:T(256)S(1)}, f32[256]{0:T(256)S(1)}, u32[]{:S(2)}, u32[]{:S(2)}) %collective-permute-start.6) | collective-permute-done | bytes 1056 | tf_op jit(solution)/shard_map/ppermute | solution.py:33
  53.4 0.7 constant_dynamic-update-slice_fusion
  54.1 0.1 fusion.5
  54.2 1.6 multiply_reduce_fusion
  55.8 11.5 %fusion = (f32[1024]{0:T(1024)S(1)}, f32[1024,2048]{1,0:T(8,128)}) fusion(f32[2048]{0:T(1024)S(1)} %fusion.5, f32[1024,128]{1,0:T(8,128)} %param.5, f32[2048,128]{1,0:T(8,128)} %all-gather.2.cloned.1.call-done, f32[2048]{0:T(1024)S(1)} %multiply_reduce_fusion, f32[1024]{0:T(1024)S(1)} %multiply_reduce_fusion.1), kind=kOutput, calls=%fused_computation.9 | convolution fusion | flops 3233807360 | bytes 9986048 | tf_op jit(solution)/shard_map/dot_general | solution.py:11
  67.3 5.6 %pmax.28 = f32[1024]{0:T(1024)S(1)} all-reduce(f32[1024]{0:T(1024)S(1)} %get-tuple-element.3), channel_id=1, replica_groups=mesh['blk'=8,'tgt'=4] {'tgt'}, use_global_device_ids=true, to_apply=%region_3.5 | all-reduce | flops 1024 | bytes 8192 | tf_op jit(solution)/shard_map/pmax | solution.py:40
  72.9 4.5 %exponential_reduce_fusion.3 = f32[1024]{0:T(1024)S(1)} fusion(f32[1024,2048]{1,0:T(8,128)} %get-tuple-element.4, f32[1024]{0:T(1024)S(1)} %get-tuple-element.3, f32[2048]{0:T(1024)S(1)} %fusion.5), kind=kLoop, calls=%fused_computation.6 | loop fusion | flops 8387584 | bytes 8404992 | tf_op jit(solution)/shard_map/reduce_sum | solution.py:39
  77.5 6.8 %psum.14 = f32[1024]{0:T(1024)S(1)} all-reduce(f32[1024]{0:T(1024)S(1)} %exponential_multiply_fusion.1), channel_id=1, replica_groups=mesh['blk'=8,'tgt'=4] {'tgt'}, use_global_device_ids=true, to_apply=%region_5.7 | all-reduce | flops 1024 | bytes 8192 | tf_op jit(solution)/shard_map/psum | solution.py:41
  84.3 4.3 %fusion.1 = f32[2048]{0:T(1024)S(1)} fusion(f32[1024,2048]{1,0:T(8,128)} %get-tuple-element.4, f32[1024]{0:T(1024)S(1)} %multiply_subtract_fusion.2), kind=kLoop, calls=%fused_computation.10 | loop fusion | flops 6289408 | bytes 8400896 | tf_op jit(solution)/shard_map/reduce_max | solution.py:45
  88.6 18.1 %pmax.29 = f32[2048]{0:T(1024)S(1)} all-reduce(f32[2048]{0:T(1024)S(1)} %fusion.1), channel_id=1, replica_groups=mesh['blk'=8,'tgt'=4] {'blk'}, use_global_device_ids=true, to_apply=%region_7.9 | all-reduce | flops 2048 | bytes 16384 | tf_op jit(solution)/shard_map/pmax | solution.py:45
  106.7 4.5 %exponential_reduce_fusion.2 = f32[2048]{0:T(1024)S(1)} fusion(f32[1024,2048]{1,0:T(8,128)} %get-tuple-element.4, f32[2048]{0:T(1024)S(1)} %pmax.29, f32[1024]{0:T(1024)S(1)} %multiply_subtract_fusion.2), kind=kLoop, calls=%fused_computation.4 | loop fusion | flops 8386560 | bytes 8409088 | tf_op jit(solution)/shard_map/reduce_sum | solution.py:46
  111.3 18.6 %all-reduce = f32[2048]{0:T(1024)S(1)} all-reduce(f32[2048]{0:T(1024)S(1)} %exponential_reduce_fusion.2), channel_id=2, replica_groups=mesh['blk'=8,'tgt'=4] {'blk'}, use_global_device_ids=true, to_apply=%region_9.11.clone | all-reduce | flops 2048 | bytes 16384
  129.9 0.1 fusion.11
  130.0 0.8 collective-permute-start.7
  130.7 5.5 %collective-permute-done.7 = f32[256]{0:T(256)S(1)} collective-permute-done((f32[256]{0:T(256)S(1)}, f32[256]{0:T(256)S(1)}, u32[]{:S(2)}, u32[]{:S(2)}) %collective-permute-start.7) | collective-permute-done | bytes 1056 | tf_op jit(solution)/shard_map/ppermute | solution.py:33
  136.3 6.3 %collective-permute-done.8 = f32[256]{0:T(256)S(1)} collective-permute-done((f32[256]{0:T(256)S(1)}, f32[256]{0:T(256)S(1)}, u32[]{:S(2)}, u32[]{:S(2)}) %collective-permute-start.8) | collective-permute-done | bytes 1056 | tf_op jit(solution)/shard_map/ppermute | solution.py:33
  142.5 6.3 %collective-permute-done.9 = f32[256]{0:T(256)S(1)} collective-permute-done((f32[256]{0:T(256)S(1)}, f32[256]{0:T(256)S(1)}, u32[]{:S(2)}, u32[]{:S(2)}) %collective-permute-start.9) | collective-permute-done | bytes 1056 | tf_op jit(solution)/shard_map/ppermute | solution.py:33
  148.8 6.3 %collective-permute-done.10 = f32[256]{0:T(256)S(1)} collective-permute-done((f32[256]{0:T(256)S(1)}, f32[256]{0:T(256)S(1)}, u32[]{:S(2)}, u32[]{:S(2)}) %collective-permute-start.10) | collective-permute-done | bytes 1056 | tf_op jit(solution)/shard_map/ppermute | solution.py:33
  155.1 6.3 %collective-permute-done.11 = f32[256]{0:T(256)S(1)} collective-permute-done((f32[256]{0:T(256)S(1)}, f32[256]{0:T(256)S(1)}, u32[]{:S(2)}, u32[]{:S(2)}) %collective-permute-start.11) | collective-permute-done | bytes 1056 | tf_op jit(solution)/shard_map/ppermute | solution.py:33
  161.3 0.0 collective-permute-start.12
  161.3 6.3 %collective-permute-done.12 = f32[256]{0:T(256)S(1)} collective-permute-done((f32[256]{0:T(256)S(1)}, f32[256]{0:T(256)S(1)}, u32[]{:S(2)}, u32[]{:S(2)}) %collective-permute-start.12) | collective-permute-done | bytes 1056 | tf_op jit(solution)/shard_map/ppermute | solution.py:33
  167.6 0.0 collective-permute-start.13
  167.6 6.3 %collective-permute-done.13 = f32[256]{0:T(256)S(1)} collective-permute-done((f32[256]{0:T(256)S(1)}, f32[256]{0:T(256)S(1)}, u32[]{:S(2)}, u32[]{:S(2)}) %collective-permute-start.13) | collective-permute-done | bytes 1056 | tf_op jit(solution)/shard_map/ppermute | solution.py:33
  174.0 0.1 fusion.4
  174.1 4.3 %fusion.2 = f32[1024]{0:T(1024)S(1)} fusion(f32[1024,2048]{1,0:T(8,128)} %get-tuple-element.4, f32[2048]{0:T(1024)S(1)} %fusion.4), kind=kLoop, calls=%fused_computation.11 | loop fusion | flops 6290432 | bytes 8400896 | tf_op jit(solution)/shard_map/reduce_max | solution.py:38
  178.4 4.5 %exponential_reduce_fusion.1 = f32[1024]{0:T(1024)S(1)} fusion(f32[1024,2048]{1,0:T(8,128)} %get-tuple-element.4, f32[1024]{0:T(1024)S(1)} %fusion.2, f32[2048]{0:T(1024)S(1)} %fusion.4), kind=kLoop, calls=%fused_computation.2 | loop fusion | flops 8387584 | bytes 8404992 | tf_op jit(solution)/shard_map/reduce_sum | solution.py:39
  182.9 5.7 %pmax.30 = f32[1024]{0:T(1024)S(1)} all-reduce(f32[1024]{0:T(1024)S(1)} %fusion.2), channel_id=1, replica_groups=mesh['blk'=8,'tgt'=4] {'tgt'}, use_global_device_ids=true, to_apply=%region_11.13 | all-reduce | flops 1024 | bytes 8192 | tf_op jit(solution)/shard_map/pmax | solution.py:40
  188.6 6.1 %psum.15 = f32[1024]{0:T(1024)S(1)} all-reduce(f32[1024]{0:T(1024)S(1)} %exponential_multiply_fusion), channel_id=1, replica_groups=mesh['blk'=8,'tgt'=4] {'tgt'}, use_global_device_ids=true, to_apply=%region_13.15 | all-reduce | flops 1024 | bytes 8192 | tf_op jit(solution)/shard_map/psum | solution.py:41
  194.7 4.3 %fusion.3 = f32[2048]{0:T(1024)S(1)} fusion(f32[1024,2048]{1,0:T(8,128)} %get-tuple-element.4, f32[1024]{0:T(1024)S(1)} %multiply_subtract_fusion.1), kind=kLoop, calls=%fused_computation.12 | loop fusion | flops 6289408 | bytes 8400896 | tf_op jit(solution)/shard_map/reduce_max | solution.py:45
  199.0 17.4 %pmax.31 = f32[2048]{0:T(1024)S(1)} all-reduce(f32[2048]{0:T(1024)S(1)} %fusion.3), channel_id=1, replica_groups=mesh['blk'=8,'tgt'=4] {'blk'}, use_global_device_ids=true, to_apply=%region_15.17 | all-reduce | flops 2048 | bytes 16384 | tf_op jit(solution)/shard_map/pmax | solution.py:45
  216.4 4.5 %exponential_reduce_fusion = f32[2048]{0:T(1024)S(1)} fusion(f32[1024,2048]{1,0:T(8,128)} %get-tuple-element.4, f32[2048]{0:T(1024)S(1)} %pmax.31, f32[1024]{0:T(1024)S(1)} %multiply_subtract_fusion.1), kind=kLoop, calls=%fused_computation | loop fusion | flops 8386560 | bytes 8409088 | tf_op jit(solution)/shard_map/reduce_sum | solution.py:46
  220.9 19.4 %all-reduce.1 = f32[2048]{0:T(1024)S(1)} all-reduce(f32[2048]{0:T(1024)S(1)} %exponential_reduce_fusion), channel_id=3, replica_groups=mesh['blk'=8,'tgt'=4] {'blk'}, use_global_device_ids=true, to_apply=%region_17.19.clone | all-reduce | flops 2048 | bytes 16384
  240.3 0.7 fusion.8
  (30 shorter events, 0.2 us)
Async XLA Ops:
  7.2 47.1 %all-gather.2.cloned.1.call-start = ((), (), s32[]{:S(2)}) async-start(), calls=%async_computation | async-start | bytes 1179648 | tf_op jit(solution)/shard_map/all_gather | solution.py:25
  7.9 7.8 %collective-permute-start = (f32[256]{0:T(256)}, f32[256]{0:T(256)S(1)}, u32[]{:S(2)}, u32[]{:S(2)}) collective-permute-start(f32[256]{0:T(256)} %param.7), channel_id=1, source_target_pairs={{0,4},{4,8},{8,12},{12,16},{16,20},{20,24},{24,28},{28,0},{1,5},{5... | collective-permute-start | bytes 3080 | tf_op jit(solution)/shard_map/ppermute | solution.py:33
  15.7 6.3 %collective-permute-start.1 = (f32[256]{0:T(256)S(1)}, f32[256]{0:T(256)S(1)}, u32[]{:S(2)}, u32[]{:S(2)}) collective-permute-start(f32[256]{0:T(256)S(1)} %collective-permute-done), channel_id=1, source_target_pairs={{0,4},{4,8},{8,12},{12,16},{16,20},{20,24},{24,28},{28,0},{1,5},{5... | collective-permute-start | bytes 3080 | tf_op jit(solution)/shard_map/ppermute | solution.py:33
  22.0 6.3 %collective-permute-start.2 = (f32[256]{0:T(256)S(1)}, f32[256]{0:T(256)S(1)}, u32[]{:S(2)}, u32[]{:S(2)}) collective-permute-start(f32[256]{0:T(256)S(1)} %collective-permute-done.1), channel_id=1, source_target_pairs={{0,4},{4,8},{8,12},{12,16},{16,20},{20,24},{24,28},{28,0},{1,5},{5... | collective-permute-start | bytes 3080 | tf_op jit(solution)/shard_map/ppermute | solution.py:33
  28.3 6.3 %collective-permute-start.3 = (f32[256]{0:T(256)S(1)}, f32[256]{0:T(256)S(1)}, u32[]{:S(2)}, u32[]{:S(2)}) collective-permute-start(f32[256]{0:T(256)S(1)} %collective-permute-done.2), channel_id=1, source_target_pairs={{0,4},{4,8},{8,12},{12,16},{16,20},{20,24},{24,28},{28,0},{1,5},{5... | collective-permute-start | bytes 3080 | tf_op jit(solution)/shard_map/ppermute | solution.py:33
  34.5 6.3 %collective-permute-start.4 = (f32[256]{0:T(256)S(1)}, f32[256]{0:T(256)S(1)}, u32[]{:S(2)}, u32[]{:S(2)}) collective-permute-start(f32[256]{0:T(256)S(1)} %collective-permute-done.3), channel_id=1, source_target_pairs={{0,4},{4,8},{8,12},{12,16},{16,20},{20,24},{24,28},{28,0},{1,5},{5... | collective-permute-start | bytes 3080 | tf_op jit(solution)/shard_map/ppermute | solution.py:33
  40.8 6.3 %collective-permute-start.5 = (f32[256]{0:T(256)S(1)}, f32[256]{0:T(256)S(1)}, u32[]{:S(2)}, u32[]{:S(2)}) collective-permute-start(f32[256]{0:T(256)S(1)} %collective-permute-done.4), channel_id=1, source_target_pairs={{0,4},{4,8},{8,12},{12,16},{16,20},{20,24},{24,28},{28,0},{1,5},{5... | collective-permute-start | bytes 3080 | tf_op jit(solution)/shard_map/ppermute | solution.py:33
  47.1 6.3 %collective-permute-start.6 = (f32[256]{0:T(256)S(1)}, f32[256]{0:T(256)S(1)}, u32[]{:S(2)}, u32[]{:S(2)}) collective-permute-start(f32[256]{0:T(256)S(1)} %collective-permute-done.5), channel_id=1, source_target_pairs={{0,4},{4,8},{8,12},{12,16},{16,20},{20,24},{24,28},{28,0},{1,5},{5... | collective-permute-start | bytes 3080 | tf_op jit(solution)/shard_map/ppermute | solution.py:33
  130.0 6.3 %collective-permute-start.7 = (f32[256]{0:T(256)S(1)}, f32[256]{0:T(256)S(1)}, u32[]{:S(2)}, u32[]{:S(2)}) collective-permute-start(f32[256]{0:T(256)S(1)} %fusion.11), channel_id=1, source_target_pairs={{0,4},{4,8},{8,12},{12,16},{16,20},{20,24},{24,28},{28,0},{1,5},{5... | collective-permute-start | bytes 3080 | tf_op jit(solution)/shard_map/ppermute | solution.py:33
  136.3 6.3 %collective-permute-start.8 = (f32[256]{0:T(256)S(1)}, f32[256]{0:T(256)S(1)}, u32[]{:S(2)}, u32[]{:S(2)}) collective-permute-start(f32[256]{0:T(256)S(1)} %collective-permute-done.7), channel_id=1, source_target_pairs={{0,4},{4,8},{8,12},{12,16},{16,20},{20,24},{24,28},{28,0},{1,5},{5... | collective-permute-start | bytes 3080 | tf_op jit(solution)/shard_map/ppermute | solution.py:33
  142.5 6.3 %collective-permute-start.9 = (f32[256]{0:T(256)S(1)}, f32[256]{0:T(256)S(1)}, u32[]{:S(2)}, u32[]{:S(2)}) collective-permute-start(f32[256]{0:T(256)S(1)} %collective-permute-done.8), channel_id=1, source_target_pairs={{0,4},{4,8},{8,12},{12,16},{16,20},{20,24},{24,28},{28,0},{1,5},{5... | collective-permute-start | bytes 3080 | tf_op jit(solution)/shard_map/ppermute | solution.py:33
  148.8 6.3 %collective-permute-start.10 = (f32[256]{0:T(256)S(1)}, f32[256]{0:T(256)S(1)}, u32[]{:S(2)}, u32[]{:S(2)}) collective-permute-start(f32[256]{0:T(256)S(1)} %collective-permute-done.9), channel_id=1, source_target_pairs={{0,4},{4,8},{8,12},{12,16},{16,20},{20,24},{24,28},{28,0},{1,5},{5... | collective-permute-start | bytes 3080 | tf_op jit(solution)/shard_map/ppermute | solution.py:33
  155.1 6.3 %collective-permute-start.11 = (f32[256]{0:T(256)S(1)}, f32[256]{0:T(256)S(1)}, u32[]{:S(2)}, u32[]{:S(2)}) collective-permute-start(f32[256]{0:T(256)S(1)} %collective-permute-done.10), channel_id=1, source_target_pairs={{0,4},{4,8},{8,12},{12,16},{16,20},{20,24},{24,28},{28,0},{1,5},{5... | collective-permute-start | bytes 3080 | tf_op jit(solution)/shard_map/ppermute | solution.py:33
  161.3 6.3 %collective-permute-start.12 = (f32[256]{0:T(256)S(1)}, f32[256]{0:T(256)S(1)}, u32[]{:S(2)}, u32[]{:S(2)}) collective-permute-start(f32[256]{0:T(256)S(1)} %collective-permute-done.11), channel_id=1, source_target_pairs={{0,4},{4,8},{8,12},{12,16},{16,20},{20,24},{24,28},{28,0},{1,5},{5... | collective-permute-start | bytes 3080 | tf_op jit(solution)/shard_map/ppermute | solution.py:33
  167.6 6.3 %collective-permute-start.13 = (f32[256]{0:T(256)S(1)}, f32[256]{0:T(256)S(1)}, u32[]{:S(2)}, u32[]{:S(2)}) collective-permute-start(f32[256]{0:T(256)S(1)} %collective-permute-done.12), channel_id=1, source_target_pairs={{0,4},{4,8},{8,12},{12,16},{16,20},{20,24},{24,28},{28,0},{1,5},{5... | collective-permute-start | bytes 3080 | tf_op jit(solution)/shard_map/ppermute | solution.py:33
  194.7 26.2 %copy-start = (f32[1024]{0:T(1024)}, f32[1024]{0:T(1024)S(1)}, u32[]{:S(2)}) copy-start(f32[1024]{0:T(1024)S(1)} %multiply_subtract_fusion.1) | copy-start | bytes 12292
Sparse Core Ops, SparseCore 0:
  10.1 43.0 all-gather.1
